TPU v7x, 32 devices: a whole 2x2x4 slice. The times are simulated.
32 devices in a mesh: gx: 4 (over z), gy: 4 (over y, x), gz: 2 (over core).
Axes of the slice: x: 2, y: 2, z: 4, core: 2. Of those that a mesh axis runs over, the one named last changes fastest.
Arguments:
- schur: bfloat16 [4, 4, 2, 2048, 2048], P('gx', 'gy', 'gz'), may hold values from -0.09375 to 0.09375
- interface_diag: float32 [4, 4, 2, 2048], P('gx', 'gy', 'gz'), may hold values from 2 to 4
- precond: float32 [4, 4, 2, 16, 128, 128], P('gx', 'gy', 'gz'), may hold values from -0.3 to 0.8
- load: bfloat16 [4, 4, 2, 2048, 256], P('gx', 'gy', 'gz'), may hold values from -170 to 170
- face_blocks: int32 [4, 4, 2, 6, 2], P('gx', 'gy', 'gz'), may hold values from 0 to 16, as said below
Outputs:
- solution: float32 [4, 4, 2, 2048, 256], P('gx', 'gy', 'gz')
- residual_norm: float32 [256], replicated
Inputs may be any that keep to these rules, and one draw needn't show every extreme that they name: `face_blocks`: for each subdomain p and direction d (0, 1: next and previous along the first grid dimension; 2, 3 and 4, 5 likewise along the second and third), slots 0 to n - 1 hold block numbers below 16 shared with the neighbour in that direction, where n (1 to 2 inside the grid, 0 across its boundary) equals the neighbour's n for the opposite direction, and the neighbour's slot k of the opposite direction holds the block that shares with p's slot k; the remaining slots hold 16; no block number appears twice in one subdomain's table; some face shares 2 blocks in every draw.
All inputs are finite; a program needn't handle non-finite values.
Results may differ from a plain program's by a relative error of at most 0.0008.
Values sent between devices are 32-bit elements; how exact they have to be, the bound alone decides.
A program may use at most 128 MiB of HBM per device.

v0:
```python
import jax
import jax.numpy as jnp
from jax import lax
from jax.sharding import PartitionSpec as P

epsilon = 1e-06


def extended_2(value, sides, width):
    for axis, dim in sides:
        peers, length = (lax.axis_size(axis), value.shape[dim])
        up = [(i, (i + 1) % peers) for i in range(peers - 1)]
        down = [(j, i) for i, j in up]
        last = lax.slice_in_dim(value, length - width, length, axis=dim)
        leading = lax.slice_in_dim(value, 0, width, axis=dim)
        before = lax.ppermute(last, axis, up)
        after = lax.ppermute(leading, axis, down)
        value = jnp.concatenate([before, value, after], axis=dim)
    return value


def assemble(blocks, slot_index, live_mask):
    block_count, block_rows, row_width = blocks.shape
    slot_count = slot_index.shape[1]
    extended = jnp.concatenate([blocks, jnp.zeros((1, block_rows, row_width), jnp.float32)], axis=0)
    slot_flat = slot_index.reshape(-1)
    packed = extended[slot_flat].reshape(6, slot_count, block_rows, row_width)
    gx_faces = extended_2(jnp.stack([packed[1], packed[0]], 0), (("gx", 0),), 1)
    gy_faces = extended_2(jnp.stack([packed[3], packed[2]], 0), (("gy", 0),), 1)
    gz_faces = extended_2(jnp.stack([packed[5], packed[4]], 0), (("gz", 0),), 1)
    arrived = jnp.stack(
        [gx_faces[3], gx_faces[0], gy_faces[3], gy_faces[0], gz_faces[3], gz_faces[0]], 0
    )
    extended = extended.at[slot_flat].add(arrived.reshape(6 * slot_count, block_rows, row_width))
    return extended[:block_count] * live_mask[:, None, None]


def partial_product(left_vec, right_vec):
    return 0.5 * jnp.sum(left_vec * right_vec, axis=(0, 1))


def on_device(schur, interface_diag, precond, load, face_blocks):
    block_count = precond.shape[3]
    block_rows = precond.shape[4]
    rhs_count = load.shape[-1]
    slot_index = face_blocks.reshape(6, face_blocks.shape[-1])
    slot_hits = slot_index[:, :, None] == jnp.arange(block_count, dtype=jnp.int32)
    live_mask = jnp.any(slot_hits, axis=(0, 1)).astype(jnp.float32)
    matrix = schur.reshape(schur.shape[-2], schur.shape[-1])
    diag_column = interface_diag.reshape(-1, 1)
    local_blocks = precond.reshape(block_count, block_rows, block_rows)
    assembled_load = assemble(
        load.reshape(block_count, block_rows, rhs_count).astype(jnp.float32), slot_index, live_mask
    )

    def precondition(vector):
        partial_value = jnp.einsum(
            "bij,bjr->bir", local_blocks, vector, precision=lax.Precision.HIGHEST
        )
        return assemble(partial_value, slot_index, live_mask)

    def operate(vector):
        flattened = vector.reshape(block_count * block_rows, rhs_count)
        narrow = flattened.astype(jnp.bfloat16)
        product = jnp.dot(matrix, narrow, preferred_element_type=jnp.float32)
        partial_value = product + diag_column * flattened
        return assemble(
            partial_value.reshape(block_count, block_rows, rhs_count), slot_index, live_mask
        )

    precond_raw = precondition(assembled_load)
    working_raw = operate(precond_raw)
    load_square, cross_first, raw_square = lax.psum(
        (
            partial_product(assembled_load, assembled_load),
            partial_product(working_raw, assembled_load),
            partial_product(working_raw, working_raw),
        ),
        ("gx", "gy", "gz"),
    )
    initial = jnp.sqrt(load_square + epsilon)
    rescale = 1.0 / initial
    basis_first = assembled_load * rescale
    precond_first = precond_raw * rescale
    diag_first = cross_first * rescale * rescale
    working = working_raw * rescale - diag_first * basis_first
    below_first = jnp.sqrt(
        jnp.maximum(raw_square * rescale * rescale - diag_first * diag_first, 0.0) + epsilon
    )
    basis_second = working / below_first
    precond_second = precondition(basis_second)
    working = operate(precond_second)
    upper_second, diag_second, work_square = lax.psum(
        (
            partial_product(working, basis_first),
            partial_product(working, basis_second),
            partial_product(working, working),
        ),
        ("gx", "gy", "gz"),
    )
    below_second = jnp.sqrt(
        jnp.maximum(work_square - upper_second * upper_second - diag_second * diag_second, 0.0)
        + epsilon
    )
    radius_first = jnp.sqrt(diag_first * diag_first + below_first * below_first)
    cosine_first = diag_first / radius_first
    sine_first = below_first / radius_first
    rotated_top = cosine_first * upper_second + sine_first * diag_second
    rotated_low = cosine_first * diag_second - sine_first * upper_second
    radius_second = jnp.sqrt(rotated_low * rotated_low + below_second * below_second)
    cosine_second = rotated_low / radius_second
    sine_second = below_second / radius_second
    weight_second = -initial * sine_first * cosine_second / radius_second
    weight_first = (initial * cosine_first - rotated_top * weight_second) / radius_first
    solution = weight_first * precond_first + weight_second * precond_second
    residual_norm = initial * sine_first * sine_second
    return (solution.reshape(1, 1, 1, block_count * block_rows, rhs_count), residual_norm)


def solution(mesh):
    placed = (
        P("gx", "gy", "gz", None, None),
        P("gx", "gy", "gz", None),
        P("gx", "gy", "gz", None, None, None),
        P("gx", "gy", "gz", None, None),
        P("gx", "gy", "gz", None, None),
    )
    return jax.shard_map(
        on_device,
        mesh=mesh,
        in_specs=placed,
        out_specs=(P("gx", "gy", "gz", None, None), P()),
        check_vma=False,
    )
```

profile of v0, /device:TPU:0, one launch (start us, length us, event | category | flops | bytes accessed | tf_op | source)
XLA Modules:
  0.0 332.8 jit_solution(5682009236857555295)
XLA Ops:
  7.7 5.6 %collective-permute-start.1 = (f32[1,2,128,256]{3,2,1,0:T(8,128)S(1)}, f32[1,2,128,256]{3,2,1,0:T(8,128)S(1)}, u32[]{:S(2)}, u32[]{:S(2)}) collective-permute-start(f32[1,2,128,256]{3,2,1,0:T(8,128)S(1)} %get-tuple-element.51), channel_id=1, source_target_pairs={{0,8},{8,16},{16,24},{1,9},{9,17},{17,25},{2,10},{10,18},{18,26},{... | collective-permute-start | bytes 786440 | tf_op jit(solution)/shard_map/ppermute | solution.py:16
  17.6 4.4 %collective-permute-start.3 = (f32[1,2,128,256]{3,2,1,0:T(8,128)S(1)}, f32[1,2,128,256]{3,2,1,0:T(8,128)S(1)}, u32[]{:S(2)}, u32[]{:S(2)}) collective-permute-start(f32[1,2,128,256]{3,2,1,0:T(8,128)S(1)} %get-tuple-element.49), channel_id=1, source_target_pairs={{0,2},{2,4},{4,6},{1,3},{3,5},{5,7},{8,10},{10,12},{12,14},{9,11},... | collective-permute-start | bytes 786440 | tf_op jit(solution)/shard_map/ppermute | solution.py:16
  22.1 4.8 %collective-permute-done.2 = f32[1,2,128,256]{3,2,1,0:T(8,128)S(1)} collective-permute-done((f32[1,2,128,256]{3,2,1,0:T(8,128)S(1)}, f32[1,2,128,256]{3,2,1,0:T(8,128)S(1)}, u32[]{:S(2)}, u32[]{:S(2)}) %collective-permute-start.2) | collective-permute-done | bytes 262176 | tf_op jit(solution)/shard_map/ppermute | solution.py:17
  33.0 3.8 %convolution_bitcast_fusion.1 = f32[16,128,256]{1,2,0:T(8,128)S(1)} fusion(f32[17,128,256]{2,1,0:T(8,128)S(1)} %scatter_fusion, f32[1,1,1,16,128,128]{5,4,3,2,1,0:T(8,128)S(1)} %copy-done, f32[16]{0:T(128)S(1)} %convert_element_type.24), kind=kOutput, calls=%fused_computation.32 | convolution fusion | flops 805830656 | bytes 5243392 | tf_op jit(solution)/shard_map/bij,bjr->bir/dot_general | solution.py:57
  38.5 3.4 %gather_fusion.1 = f32[12,128,256]{1,2,0:T(8,128)} fusion(f32[17,128,256]{1,2,0:T(8,128)} %concatenate.19, s32[1024]{0:T(1024)S(1)} %pad_clamp_fusion), kind=kCustom, calls=%fused_computation.1 | custom fusion | bytes 3145776 | tf_op jit(solution)/shard_map/gather | solution.py:27
  45.6 5.3 %collective-permute-start.7 = (f32[1,2,128,256]{2,3,1,0:T(8,128)}, f32[1,2,128,256]{2,3,1,0:T(8,128)}, u32[]{:S(2)}, u32[]{:S(2)}) collective-permute-start(f32[1,2,128,256]{2,3,1,0:T(8,128)} %get-tuple-element.45), channel_id=1, source_target_pairs={{0,8},{8,16},{16,24},{1,9},{9,17},{17,25},{2,10},{10,18},{18,26},{... | collective-permute-start | bytes 786440 | tf_op jit(solution)/shard_map/ppermute | solution.py:16
  57.9 6.6 %collective-permute-start.9 = (f32[1,2,128,256]{2,3,1,0:T(8,128)}, f32[1,2,128,256]{2,3,1,0:T(8,128)S(1)}, u32[]{:S(2)}, u32[]{:S(2)}) collective-permute-start(f32[1,2,128,256]{2,3,1,0:T(8,128)} %get-tuple-element.43), channel_id=1, source_target_pairs={{0,2},{2,4},{4,6},{1,3},{3,5},{5,7},{8,10},{10,12},{12,14},{9,11},... | collective-permute-start | bytes 786440 | tf_op jit(solution)/shard_map/ppermute | solution.py:16
  76.3 4.5 %scatter_fusion.1 = f32[17,128,256]{2,1,0:T(8,128)} fusion(f32[17,128,256]{2,1,0:T(8,128)} %copy.23, s32[12]{0:T(128)S(1)} %fusion.24, f32[12,128,256]{2,1,0:T(8,128)} %copy.24), kind=kCustom, calls=%fused_computation.6 | custom fusion | flops 393216 | bytes 4718640 | tf_op jit(solution)/shard_map/scatter-add | solution.py:34
  80.8 3.6 %fusion.28 = (bf16[16,128,256]{2,1,0:T(8,128)(2,1)}, f32[16,128,256]{2,1,0:T(8,128)}) fusion(f32[16]{0:T(128)S(1)} %convert_element_type.24, f32[17,128,256]{2,1,0:T(8,128)} %scatter_fusion.1), kind=kLoop, calls=%fused_computation.126 | loop fusion | flops 1048576 | bytes 5242944 | tf_op jit(solution)/shard_map/convert_element_type | solution.py:64
  87.3 8.0 %fusion.13 = f32[2048,256]{0,1:T(8,128)} fusion(bf16[2048,256]{1,0:T(8,128)(2,1)} %bitcast.116, bf16[1,1,1,2048,2048]{4,3,2,1,0:T(8,128)(2,1)} %param.5, f32[2048,256]{0,1:T(8,128)} %copy.25, f32[2048]{0:T(1024)S(1)} %bitcast.119), kind=kOutput, calls=%fused_computation.17 | convolution fusion | flops 2148532224 | bytes 13639680 | tf_op jit(solution)/shard_map/dot_general | solution.py:65
  101.4 3.4 %gather_fusion.2 = f32[12,128,256]{2,1,0:T(8,128)} fusion(f32[17,128,256]{2,1,0:T(8,128)} %concatenate.20, s32[1024]{0:T(1024)S(1)} %pad_clamp_fusion), kind=kCustom, calls=%fused_computation.2 | custom fusion | bytes 3145776 | tf_op jit(solution)/shard_map/gather | solution.py:27
  107.7 4.6 %collective-permute-start.13 = (f32[1,2,128,256]{3,2,1,0:T(8,128)S(1)}, f32[1,2,128,256]{3,2,1,0:T(8,128)S(1)}, u32[]{:S(2)}, u32[]{:S(2)}) collective-permute-start(f32[1,2,128,256]{3,2,1,0:T(8,128)S(1)} %get-tuple-element.39), channel_id=1, source_target_pairs={{0,8},{8,16},{16,24},{1,9},{9,17},{17,25},{2,10},{10,18},{18,26},{... | collective-permute-start | bytes 786440 | tf_op jit(solution)/shard_map/ppermute | solution.py:16
  116.7 5.5 %collective-permute-start.15 = (f32[1,2,128,256]{3,2,1,0:T(8,128)S(1)}, f32[1,2,128,256]{3,2,1,0:T(8,128)S(1)}, u32[]{:S(2)}, u32[]{:S(2)}) collective-permute-start(f32[1,2,128,256]{3,2,1,0:T(8,128)S(1)} %get-tuple-element.37), channel_id=1, source_target_pairs={{0,2},{2,4},{4,6},{1,3},{3,5},{5,7},{8,10},{10,12},{12,14},{9,11},... | collective-permute-start | bytes 786440 | tf_op jit(solution)/shard_map/ppermute | solution.py:16
  124.4 4.3 %collective-permute-done.15 = f32[1,2,128,256]{3,2,1,0:T(8,128)S(1)} collective-permute-done((f32[1,2,128,256]{3,2,1,0:T(8,128)S(1)}, f32[1,2,128,256]{3,2,1,0:T(8,128)S(1)}, u32[]{:S(2)}, u32[]{:S(2)}) %collective-permute-start.15) | collective-permute-done | bytes 262176 | tf_op jit(solution)/shard_map/ppermute | solution.py:16
  130.9 4.5 %scatter_fusion.2 = f32[17,128,256]{2,1,0:T(8,128)} fusion(f32[17,128,256]{2,1,0:T(8,128)} %concatenate.20, s32[12]{0:T(128)S(1)} %fusion.24, f32[12,128,256]{2,1,0:T(8,128)} %bitcast.31), kind=kCustom, calls=%fused_computation.7 | custom fusion | flops 393216 | bytes 4718640 | tf_op jit(solution)/shard_map/scatter-add | solution.py:34
  137.7 44.0 %all-reduce.6 = (f32[256]{0:T(256)S(1)}, f32[256]{0:T(256)S(1)}, f32[256]{0:T(256)S(1)}) all-reduce(f32[256]{0:T(256)S(1)} %broadcast_multiply_fusion.5, f32[256]{0:T(256)S(1)} %get-tuple-element.54, f32[256]{0:T(256)S(1)} %get-tuple-element.55), channel_id=1, replica_groups=mesh['gx'=4,'gy'=4,'gz'=2] {'gx','gy','gz'}, use_global_device_ids=true, to_apply=%region_3.0 | all-reduce | flops 768 | bytes 6144 | tf_op jit(solution)/shard_map/psum | solution.py:73
  181.7 5.7 %convolution_bitcast_fusion = f32[16,128,256]{1,2,0:T(8,128)S(1)} fusion(f32[1,1,1,16,128,128]{5,4,3,2,1,0:T(8,128)S(1)} %copy-done, f32[17,128,256]{2,1,0:T(8,128)} %scatter_fusion.2, f32[17,128,256]{2,1,0:T(8,128)S(1)} %scatter_fusion, f32[256]{0:T(256)S(1)} %get-tuple-element.18, f32[256]{0:T(256)S(1)} %get-tuple-element.19, ...), kind=kOutput, calls=%fused_computation.31 | convolution fusion | flops 808976384 | bytes 7343616 | tf_op jit(solution)/shard_map/bij,bjr->bir/dot_general | solution.py:57
  189.1 3.4 %gather_fusion.3 = f32[12,128,256]{1,2,0:T(8,128)} fusion(f32[17,128,256]{1,2,0:T(8,128)} %concatenate.21, s32[1024]{0:T(1024)S(1)} %pad_clamp_fusion), kind=kCustom, calls=%fused_computation.3 | custom fusion | bytes 3145776 | tf_op jit(solution)/shard_map/gather | solution.py:27
  195.9 5.3 %collective-permute-start.19 = (f32[1,2,128,256]{2,3,1,0:T(8,128)S(1)}, f32[1,2,128,256]{2,3,1,0:T(8,128)}, u32[]{:S(2)}, u32[]{:S(2)}) collective-permute-start(f32[1,2,128,256]{2,3,1,0:T(8,128)S(1)} %get-tuple-element.33), channel_id=1, source_target_pairs={{0,8},{8,16},{16,24},{1,9},{9,17},{17,25},{2,10},{10,18},{18,26},{... | collective-permute-start | bytes 786440 | tf_op jit(solution)/shard_map/ppermute | solution.py:16
  208.1 4.8 %collective-permute-start.21 = (f32[1,2,128,256]{2,3,1,0:T(8,128)S(1)}, f32[1,2,128,256]{2,3,1,0:T(8,128)S(1)}, u32[]{:S(2)}, u32[]{:S(2)}) collective-permute-start(f32[1,2,128,256]{2,3,1,0:T(8,128)S(1)} %get-tuple-element.31), channel_id=1, source_target_pairs={{0,2},{2,4},{4,6},{1,3},{3,5},{5,7},{8,10},{10,12},{12,14},{9,11},... | collective-permute-start | bytes 786440 | tf_op jit(solution)/shard_map/ppermute | solution.py:16
  224.7 4.5 %scatter_fusion.3 = f32[17,128,256]{2,1,0:T(8,128)} fusion(f32[17,128,256]{2,1,0:T(8,128)} %copy.28, s32[12]{0:T(128)S(1)} %fusion.24, f32[12,128,256]{2,1,0:T(8,128)} %copy.29), kind=kCustom, calls=%fused_computation.8 | custom fusion | flops 393216 | bytes 4718640 | tf_op jit(solution)/shard_map/scatter-add | solution.py:34
  229.2 3.3 fusion.27
  235.4 7.7 %fusion.10 = f32[2048,256]{0,1:T(8,128)} fusion(bf16[2048,256]{1,0:T(8,128)(2,1)S(1)} %bitcast.117, bf16[1,1,1,2048,2048]{4,3,2,1,0:T(8,128)(2,1)} %param.5, f32[2048,256]{0,1:T(8,128)} %copy.30, f32[2048]{0:T(1024)S(1)} %bitcast.120), kind=kOutput, calls=%fused_computation.16 | convolution fusion | flops 2148532224 | bytes 13639680 | tf_op jit(solution)/shard_map/dot_general | solution.py:65
  246.1 3.2 concatenate.22
  249.3 3.4 %gather_fusion.4 = f32[12,128,256]{2,1,0:T(8,128)} fusion(f32[17,128,256]{2,1,0:T(8,128)} %concatenate.22, s32[1024]{0:T(1024)S(1)} %pad_clamp_fusion), kind=kCustom, calls=%fused_computation.4 | custom fusion | bytes 3145776 | tf_op jit(solution)/shard_map/gather | solution.py:27
  255.5 4.6 %collective-permute-start.25 = (f32[1,2,128,256]{3,2,1,0:T(8,128)S(1)}, f32[1,2,128,256]{3,2,1,0:T(8,128)S(1)}, u32[]{:S(2)}, u32[]{:S(2)}) collective-permute-start(f32[1,2,128,256]{3,2,1,0:T(8,128)S(1)} %get-tuple-element.27), channel_id=1, source_target_pairs={{0,8},{8,16},{16,24},{1,9},{9,17},{17,25},{2,10},{10,18},{18,26},{... | collective-permute-start | bytes 786440 | tf_op jit(solution)/shard_map/ppermute | solution.py:16
  264.5 5.5 %collective-permute-start.27 = (f32[1,2,128,256]{3,2,1,0:T(8,128)S(1)}, f32[1,2,128,256]{3,2,1,0:T(8,128)S(1)}, u32[]{:S(2)}, u32[]{:S(2)}) collective-permute-start(f32[1,2,128,256]{3,2,1,0:T(8,128)S(1)} %get-tuple-element.25), channel_id=1, source_target_pairs={{0,2},{2,4},{4,6},{1,3},{3,5},{5,7},{8,10},{10,12},{12,14},{9,11},... | collective-permute-start | bytes 786440 | tf_op jit(solution)/shard_map/ppermute | solution.py:16
  272.2 4.0 %collective-permute-done.27 = f32[1,2,128,256]{3,2,1,0:T(8,128)S(1)} collective-permute-done((f32[1,2,128,256]{3,2,1,0:T(8,128)S(1)}, f32[1,2,128,256]{3,2,1,0:T(8,128)S(1)}, u32[]{:S(2)}, u32[]{:S(2)}) %collective-permute-start.27) | collective-permute-done | bytes 262176 | tf_op jit(solution)/shard_map/ppermute | solution.py:16
  278.5 4.5 %scatter_fusion.4 = f32[17,128,256]{2,1,0:T(8,128)} fusion(f32[17,128,256]{2,1,0:T(8,128)} %concatenate.22, s32[12]{0:T(128)S(1)} %fusion.24, f32[12,128,256]{2,1,0:T(8,128)} %bitcast.50), kind=kCustom, calls=%fused_computation.9 | custom fusion | flops 393216 | bytes 4718640 | tf_op jit(solution)/shard_map/scatter-add | solution.py:34
  282.9 3.2 multiply_reduce_fusion.2
  286.2 42.0 %all-reduce.5 = (f32[256]{0:T(256)S(1)}, f32[256]{0:T(256)S(1)}, f32[256]{0:T(256)S(1)}) all-reduce(f32[256]{0:T(256)S(1)} %broadcast_multiply_fusion.1, f32[256]{0:T(256)S(1)} %broadcast_multiply_fusion, f32[256]{0:T(256)S(1)} %broadcast_multiply_fusion.2), channel_id=1, replica_groups=mesh['gx'=4,'gy'=4,'gz'=2] {'gx','gy','gz'}, use_global_device_ids=true, to_apply=%region_15.0 | all-reduce | flops 768 | bytes 6144 | tf_op jit(solution)/shard_map/psum | solution.py:93
  328.9 4.0 %multiply_add_fusion = f32[16,128,256]{2,1,0:T(8,128)} fusion(f32[16,128,256]{2,1,0:T(8,128)} %get-tuple-element.17, f32[16,128,256]{2,1,0:T(8,128)} %get-tuple-element.22, f32[256]{0:T(256)S(1)} %get-tuple-element.15, f32[256]{0:T(256)S(1)} %get-tuple-element.14, f32[256]{0:T(256)S(1)} %get-tuple-element.20), kind=kLoop, calls=%fused_computation.23 | loop fusion | flops 2097152 | bytes 6294528 | tf_op jit(solution)/shard_map/add | solution.py:115
  (134 shorter events, 106.3 us)
Async XLA Ops:
  0.6 32.4 %copy-start = (f32[1,1,1,16,128,128]{5,4,3,2,1,0:T(8,128)S(1)}, f32[1,1,1,16,128,128]{5,4,3,2,1,0:T(8,128)}, u32[]{:S(2)}) copy-start(f32[1,1,1,16,128,128]{5,4,3,2,1,0:T(8,128)} %param.7) | copy-start | bytes 3145732
  6.4 11.3 %collective-permute-start = (f32[1,2,128,256]{3,2,1,0:T(8,128)S(1)}, f32[1,2,128,256]{3,2,1,0:T(8,128)S(1)}, u32[]{:S(2)}, u32[]{:S(2)}) collective-permute-start(f32[1,2,128,256]{3,2,1,0:T(8,128)S(1)} %get-tuple-element.52), channel_id=1, source_target_pairs={{8,0},{16,8},{24,16},{9,1},{17,9},{25,17},{10,2},{18,10},{26,18},{... | collective-permute-start | bytes 786440 | tf_op jit(solution)/shard_map/ppermute | solution.py:17
  7.7 14.4 %collective-permute-start.1 = (f32[1,2,128,256]{3,2,1,0:T(8,128)S(1)}, f32[1,2,128,256]{3,2,1,0:T(8,128)S(1)}, u32[]{:S(2)}, u32[]{:S(2)}) collective-permute-start(f32[1,2,128,256]{3,2,1,0:T(8,128)S(1)} %get-tuple-element.51), channel_id=1, source_target_pairs={{0,8},{8,16},{16,24},{1,9},{9,17},{17,25},{2,10},{10,18},{18,26},{... | collective-permute-start | bytes 786440 | tf_op jit(solution)/shard_map/ppermute | solution.py:16
  13.3 15.4 %collective-permute-start.5 = (f32[1,2,128,256]{3,2,1,0:T(8,128)S(1)}, f32[1,2,128,256]{3,2,1,0:T(8,128)S(1)}, u32[]{:S(2)}, u32[]{:S(2)}) collective-permute-start(f32[1,2,128,256]{3,2,1,0:T(8,128)S(1)} %get-tuple-element.47), channel_id=1, source_target_pairs={{0,1},{2,3},{4,5},{6,7},{8,9},{10,11},{12,13},{14,15},{16,17},{18,... | collective-permute-start | bytes 786440 | tf_op jit(solution)/shard_map/ppermute | solution.py:16
  14.8 13.9 %collective-permute-start.4 = (f32[1,2,128,256]{3,2,1,0:T(8,128)S(1)}, f32[1,2,128,256]{3,2,1,0:T(8,128)S(1)}, u32[]{:S(2)}, u32[]{:S(2)}) collective-permute-start(f32[1,2,128,256]{3,2,1,0:T(8,128)S(1)} %get-tuple-element.48), channel_id=1, source_target_pairs={{1,0},{3,2},{5,4},{7,6},{9,8},{11,10},{13,12},{15,14},{17,16},{19,... | collective-permute-start | bytes 786440 | tf_op jit(solution)/shard_map/ppermute | solution.py:17
  16.1 10.9 %collective-permute-start.2 = (f32[1,2,128,256]{3,2,1,0:T(8,128)S(1)}, f32[1,2,128,256]{3,2,1,0:T(8,128)S(1)}, u32[]{:S(2)}, u32[]{:S(2)}) collective-permute-start(f32[1,2,128,256]{3,2,1,0:T(8,128)S(1)} %get-tuple-element.50), channel_id=1, source_target_pairs={{2,0},{4,2},{6,4},{3,1},{5,3},{7,5},{10,8},{12,10},{14,12},{11,9},... | collective-permute-start | bytes 786440 | tf_op jit(solution)/shard_map/ppermute | solution.py:17
  17.6 11.0 %collective-permute-start.3 = (f32[1,2,128,256]{3,2,1,0:T(8,128)S(1)}, f32[1,2,128,256]{3,2,1,0:T(8,128)S(1)}, u32[]{:S(2)}, u32[]{:S(2)}) collective-permute-start(f32[1,2,128,256]{3,2,1,0:T(8,128)S(1)} %get-tuple-element.49), channel_id=1, source_target_pairs={{0,2},{2,4},{4,6},{1,3},{3,5},{5,7},{8,10},{10,12},{12,14},{9,11},... | collective-permute-start | bytes 786440 | tf_op jit(solution)/shard_map/ppermute | solution.py:16
  44.3 13.6 %collective-permute-start.6 = (f32[1,2,128,256]{2,3,1,0:T(8,128)}, f32[1,2,128,256]{2,3,1,0:T(8,128)}, u32[]{:S(2)}, u32[]{:S(2)}) collective-permute-start(f32[1,2,128,256]{2,3,1,0:T(8,128)} %get-tuple-element.46), channel_id=1, source_target_pairs={{8,0},{16,8},{24,16},{9,1},{17,9},{25,17},{10,2},{18,10},{26,18},{... | collective-permute-start | bytes 786440 | tf_op jit(solution)/shard_map/ppermute | solution.py:17
  45.6 20.5 %collective-permute-start.7 = (f32[1,2,128,256]{2,3,1,0:T(8,128)}, f32[1,2,128,256]{2,3,1,0:T(8,128)}, u32[]{:S(2)}, u32[]{:S(2)}) collective-permute-start(f32[1,2,128,256]{2,3,1,0:T(8,128)} %get-tuple-element.45), channel_id=1, source_target_pairs={{0,8},{8,16},{16,24},{1,9},{9,17},{17,25},{2,10},{10,18},{18,26},{... | collective-permute-start | bytes 786440 | tf_op jit(solution)/shard_map/ppermute | solution.py:16
  50.9 17.0 %collective-permute-start.8 = (f32[1,2,128,256]{2,3,1,0:T(8,128)}, f32[1,2,128,256]{2,3,1,0:T(8,128)}, u32[]{:S(2)}, u32[]{:S(2)}) collective-permute-start(f32[1,2,128,256]{2,3,1,0:T(8,128)} %get-tuple-element.44), channel_id=1, source_target_pairs={{2,0},{4,2},{6,4},{3,1},{5,3},{7,5},{10,8},{12,10},{14,12},{11,9},... | collective-permute-start | bytes 786440 | tf_op jit(solution)/shard_map/ppermute | solution.py:17
  55.2 17.4 %collective-permute-start.11 = (f32[1,2,128,256]{2,3,1,0:T(8,128)S(1)}, f32[1,2,128,256]{2,3,1,0:T(8,128)S(1)}, u32[]{:S(2)}, u32[]{:S(2)}) collective-permute-start(f32[1,2,128,256]{2,3,1,0:T(8,128)S(1)} %get-tuple-element.41), channel_id=1, source_target_pairs={{0,1},{2,3},{4,5},{6,7},{8,9},{10,11},{12,13},{14,15},{16,17},{18,... | collective-permute-start | bytes 786440 | tf_op jit(solution)/shard_map/ppermute | solution.py:16
  56.6 15.2 %collective-permute-start.10 = (f32[1,2,128,256]{2,3,1,0:T(8,128)}, f32[1,2,128,256]{2,3,1,0:T(8,128)S(1)}, u32[]{:S(2)}, u32[]{:S(2)}) collective-permute-start(f32[1,2,128,256]{2,3,1,0:T(8,128)} %get-tuple-element.42), channel_id=1, source_target_pairs={{1,0},{3,2},{5,4},{7,6},{9,8},{11,10},{13,12},{15,14},{17,16},{19,... | collective-permute-start | bytes 786440 | tf_op jit(solution)/shard_map/ppermute | solution.py:17
  57.9 13.2 %collective-permute-start.9 = (f32[1,2,128,256]{2,3,1,0:T(8,128)}, f32[1,2,128,256]{2,3,1,0:T(8,128)S(1)}, u32[]{:S(2)}, u32[]{:S(2)}) collective-permute-start(f32[1,2,128,256]{2,3,1,0:T(8,128)} %get-tuple-element.43), channel_id=1, source_target_pairs={{0,2},{2,4},{4,6},{1,3},{3,5},{5,7},{8,10},{10,12},{12,14},{9,11},... | collective-permute-start | bytes 786440 | tf_op jit(solution)/shard_map/ppermute | solution.py:16
  106.4 10.3 %collective-permute-start.12 = (f32[1,2,128,256]{3,2,1,0:T(8,128)S(1)}, f32[1,2,128,256]{3,2,1,0:T(8,128)S(1)}, u32[]{:S(2)}, u32[]{:S(2)}) collective-permute-start(f32[1,2,128,256]{3,2,1,0:T(8,128)S(1)} %get-tuple-element.40), channel_id=1, source_target_pairs={{8,0},{16,8},{24,16},{9,1},{17,9},{25,17},{10,2},{18,10},{26,18},{... | collective-permute-start | bytes 786440 | tf_op jit(solution)/shard_map/ppermute | solution.py:17
  107.7 15.3 %collective-permute-start.13 = (f32[1,2,128,256]{3,2,1,0:T(8,128)S(1)}, f32[1,2,128,256]{3,2,1,0:T(8,128)S(1)}, u32[]{:S(2)}, u32[]{:S(2)}) collective-permute-start(f32[1,2,128,256]{3,2,1,0:T(8,128)S(1)} %get-tuple-element.39), channel_id=1, source_target_pairs={{0,8},{8,16},{16,24},{1,9},{9,17},{17,25},{2,10},{10,18},{18,26},{... | collective-permute-start | bytes 786440 | tf_op jit(solution)/shard_map/ppermute | solution.py:16
  112.2 11.4 %collective-permute-start.14 = (f32[1,2,128,256]{3,2,1,0:T(8,128)S(1)}, f32[1,2,128,256]{3,2,1,0:T(8,128)S(1)}, u32[]{:S(2)}, u32[]{:S(2)}) collective-permute-start(f32[1,2,128,256]{3,2,1,0:T(8,128)S(1)} %get-tuple-element.38), channel_id=1, source_target_pairs={{2,0},{4,2},{6,4},{3,1},{5,3},{7,5},{10,8},{12,10},{14,12},{11,9},... | collective-permute-start | bytes 786440 | tf_op jit(solution)/shard_map/ppermute | solution.py:17
  113.5 16.7 %collective-permute-start.17 = (f32[1,2,128,256]{3,2,1,0:T(8,128)S(1)}, f32[1,2,128,256]{3,2,1,0:T(8,128)S(1)}, u32[]{:S(2)}, u32[]{:S(2)}) collective-permute-start(f32[1,2,128,256]{3,2,1,0:T(8,128)S(1)} %get-tuple-element.35), channel_id=1, source_target_pairs={{0,1},{2,3},{4,5},{6,7},{8,9},{10,11},{12,13},{14,15},{16,17},{18,... | collective-permute-start | bytes 786440 | tf_op jit(solution)/shard_map/ppermute | solution.py:16
  115.2 14.3 %collective-permute-start.16 = (f32[1,2,128,256]{3,2,1,0:T(8,128)S(1)}, f32[1,2,128,256]{3,2,1,0:T(8,128)S(1)}, u32[]{:S(2)}, u32[]{:S(2)}) collective-permute-start(f32[1,2,128,256]{3,2,1,0:T(8,128)S(1)} %get-tuple-element.36), channel_id=1, source_target_pairs={{1,0},{3,2},{5,4},{7,6},{9,8},{11,10},{13,12},{15,14},{17,16},{19,... | collective-permute-start | bytes 786440 | tf_op jit(solution)/shard_map/ppermute | solution.py:17
  116.7 12.0 %collective-permute-start.15 = (f32[1,2,128,256]{3,2,1,0:T(8,128)S(1)}, f32[1,2,128,256]{3,2,1,0:T(8,128)S(1)}, u32[]{:S(2)}, u32[]{:S(2)}) collective-permute-start(f32[1,2,128,256]{3,2,1,0:T(8,128)S(1)} %get-tuple-element.37), channel_id=1, source_target_pairs={{0,2},{2,4},{4,6},{1,3},{3,5},{5,7},{8,10},{10,12},{12,14},{9,11},... | collective-permute-start | bytes 786440 | tf_op jit(solution)/shard_map/ppermute | solution.py:16
  194.6 13.5 %collective-permute-start.18 = (f32[1,2,128,256]{2,3,1,0:T(8,128)}, f32[1,2,128,256]{2,3,1,0:T(8,128)}, u32[]{:S(2)}, u32[]{:S(2)}) collective-permute-start(f32[1,2,128,256]{2,3,1,0:T(8,128)} %get-tuple-element.34), channel_id=1, source_target_pairs={{8,0},{16,8},{24,16},{9,1},{17,9},{25,17},{10,2},{18,10},{26,18},{... | collective-permute-start | bytes 786440 | tf_op jit(solution)/shard_map/ppermute | solution.py:17
  195.9 18.7 %collective-permute-start.19 = (f32[1,2,128,256]{2,3,1,0:T(8,128)S(1)}, f32[1,2,128,256]{2,3,1,0:T(8,128)}, u32[]{:S(2)}, u32[]{:S(2)}) collective-permute-start(f32[1,2,128,256]{2,3,1,0:T(8,128)S(1)} %get-tuple-element.33), channel_id=1, source_target_pairs={{0,8},{8,16},{16,24},{1,9},{9,17},{17,25},{2,10},{10,18},{18,26},{... | collective-permute-start | bytes 786440 | tf_op jit(solution)/shard_map/ppermute | solution.py:16
  201.2 15.1 %collective-permute-start.20 = (f32[1,2,128,256]{2,3,1,0:T(8,128)S(1)}, f32[1,2,128,256]{2,3,1,0:T(8,128)}, u32[]{:S(2)}, u32[]{:S(2)}) collective-permute-start(f32[1,2,128,256]{2,3,1,0:T(8,128)S(1)} %get-tuple-element.32), channel_id=1, source_target_pairs={{2,0},{4,2},{6,4},{3,1},{5,3},{7,5},{10,8},{12,10},{14,12},{11,9},... | collective-permute-start | bytes 786440 | tf_op jit(solution)/shard_map/ppermute | solution.py:17
  205.5 15.4 %collective-permute-start.23 = (f32[1,2,128,256]{2,3,1,0:T(8,128)S(1)}, f32[1,2,128,256]{2,3,1,0:T(8,128)S(1)}, u32[]{:S(2)}, u32[]{:S(2)}) collective-permute-start(f32[1,2,128,256]{2,3,1,0:T(8,128)S(1)} %get-tuple-element.29), channel_id=1, source_target_pairs={{0,1},{2,3},{4,5},{6,7},{8,9},{10,11},{12,13},{14,15},{16,17},{18,... | collective-permute-start | bytes 786440 | tf_op jit(solution)/shard_map/ppermute | solution.py:16
  206.8 13.4 %collective-permute-start.22 = (f32[1,2,128,256]{2,3,1,0:T(8,128)S(1)}, f32[1,2,128,256]{2,3,1,0:T(8,128)S(1)}, u32[]{:S(2)}, u32[]{:S(2)}) collective-permute-start(f32[1,2,128,256]{2,3,1,0:T(8,128)S(1)} %get-tuple-element.30), channel_id=1, source_target_pairs={{1,0},{3,2},{5,4},{7,6},{9,8},{11,10},{13,12},{15,14},{17,16},{19,... | collective-permute-start | bytes 786440 | tf_op jit(solution)/shard_map/ppermute | solution.py:17
  208.1 11.3 %collective-permute-start.21 = (f32[1,2,128,256]{2,3,1,0:T(8,128)S(1)}, f32[1,2,128,256]{2,3,1,0:T(8,128)S(1)}, u32[]{:S(2)}, u32[]{:S(2)}) collective-permute-start(f32[1,2,128,256]{2,3,1,0:T(8,128)S(1)} %get-tuple-element.31), channel_id=1, source_target_pairs={{0,2},{2,4},{4,6},{1,3},{3,5},{5,7},{8,10},{10,12},{12,14},{9,11},... | collective-permute-start | bytes 786440 | tf_op jit(solution)/shard_map/ppermute | solution.py:16
  254.2 10.3 %collective-permute-start.24 = (f32[1,2,128,256]{3,2,1,0:T(8,128)S(1)}, f32[1,2,128,256]{3,2,1,0:T(8,128)S(1)}, u32[]{:S(2)}, u32[]{:S(2)}) collective-permute-start(f32[1,2,128,256]{3,2,1,0:T(8,128)S(1)} %get-tuple-element.28), channel_id=1, source_target_pairs={{8,0},{16,8},{24,16},{9,1},{17,9},{25,17},{10,2},{18,10},{26,18},{... | collective-permute-start | bytes 786440 | tf_op jit(solution)/shard_map/ppermute | solution.py:17
  255.5 15.3 %collective-permute-start.25 = (f32[1,2,128,256]{3,2,1,0:T(8,128)S(1)}, f32[1,2,128,256]{3,2,1,0:T(8,128)S(1)}, u32[]{:S(2)}, u32[]{:S(2)}) collective-permute-start(f32[1,2,128,256]{3,2,1,0:T(8,128)S(1)} %get-tuple-element.27), channel_id=1, source_target_pairs={{0,8},{8,16},{16,24},{1,9},{9,17},{17,25},{2,10},{10,18},{18,26},{... | collective-permute-start | bytes 786440 | tf_op jit(solution)/shard_map/ppermute | solution.py:16
  260.1 11.4 %collective-permute-start.26 = (f32[1,2,128,256]{3,2,1,0:T(8,128)S(1)}, f32[1,2,128,256]{3,2,1,0:T(8,128)S(1)}, u32[]{:S(2)}, u32[]{:S(2)}) collective-permute-start(f32[1,2,128,256]{3,2,1,0:T(8,128)S(1)} %get-tuple-element.26), channel_id=1, source_target_pairs={{2,0},{4,2},{6,4},{3,1},{5,3},{7,5},{10,8},{12,10},{14,12},{11,9},... | collective-permute-start | bytes 786440 | tf_op jit(solution)/shard_map/ppermute | solution.py:17
  261.4 16.3 %collective-permute-start.29 = (f32[1,2,128,256]{3,2,1,0:T(8,128)S(1)}, f32[1,2,128,256]{3,2,1,0:T(8,128)S(1)}, u32[]{:S(2)}, u32[]{:S(2)}) collective-permute-start(f32[1,2,128,256]{3,2,1,0:T(8,128)S(1)} %get-tuple-element.23), channel_id=1, source_target_pairs={{0,1},{2,3},{4,5},{6,7},{8,9},{10,11},{12,13},{14,15},{16,17},{18,... | collective-permute-start | bytes 786440 | tf_op jit(solution)/shard_map/ppermute | solution.py:16
  263.0 14.0 %collective-permute-start.28 = (f32[1,2,128,256]{3,2,1,0:T(8,128)S(1)}, f32[1,2,128,256]{3,2,1,0:T(8,128)S(1)}, u32[]{:S(2)}, u32[]{:S(2)}) collective-permute-start(f32[1,2,128,256]{3,2,1,0:T(8,128)S(1)} %get-tuple-element.24), channel_id=1, source_target_pairs={{1,0},{3,2},{5,4},{7,6},{9,8},{11,10},{13,12},{15,14},{17,16},{19,... | collective-permute-start | bytes 786440 | tf_op jit(solution)/shard_map/ppermute | solution.py:17
  264.5 11.7 %collective-permute-start.27 = (f32[1,2,128,256]{3,2,1,0:T(8,128)S(1)}, f32[1,2,128,256]{3,2,1,0:T(8,128)S(1)}, u32[]{:S(2)}, u32[]{:S(2)}) collective-permute-start(f32[1,2,128,256]{3,2,1,0:T(8,128)S(1)} %get-tuple-element.25), channel_id=1, source_target_pairs={{0,2},{2,4},{4,6},{1,3},{3,5},{5,7},{8,10},{10,12},{12,14},{9,11},... | collective-permute-start | bytes 786440 | tf_op jit(solution)/shard_map/ppermute | solution.py:16
  282.9 45.3 %copy-start.8 = (f32[256]{0:T(256)S(1)}, f32[256]{0:T(256)}, u32[]{:S(2)}) copy-start(f32[256]{0:T(256)} %copy-done.7) | copy-start | bytes 3076
  (10 other events, 49.6 us)
where the time goes:
time: 335 us; the launch traced here: 333 us
  blocking collectives  86 us (26%)
  local copies, waits for them, and re-layouts  83.5 us (25%)
  starting transfers between devices  78.7 us (23%)
  other arithmetic  39.6 us (12%)
  matrix products  25.2 us (8%)
  waiting for transfers between devices  18.6 us (6%)
    ppermute x15, starting transfers between devices, extended_2(): before = lax.ppermute(last, axis, up)  59.4 us
    psum x1, blocking collectives, on_device(): lax.psum((partial_product(assembled_load, assembled_load), partial_produc...  44 us
    psum x1, blocking collectives, on_device(): lax.psum((partial_product(working, basis_first), partial_product(working,...  42 us
    unnamed x50, local copies, waits for them, and re-layouts  22.4 us
    scatter-add x5, other arithmetic, assemble(): extended.at[slot_flat]  21 us
    ppermute x15, starting transfers between devices, extended_2(): after = lax.ppermute(leading, axis, down)  19.3 us
    dot_general x2, matrix products, operate(): product = jnp.dot(matrix, narrow, preferred_element_type=jnp.float32)  15.7 us
    concatenate x6, local copies, waits for them, and re-layouts, assemble(): jnp.concatenate([blocks, jnp.zeros((1, block_rows, row_width), jnp.float3...  15.7 us
  transfers between devices with their start and end apart: 30, of which 9 were waited for; matrix products, arithmetic and copies ran while one was open for 8% of the time, Pallas kernels for 0%

commit v1 on v0

--- a/solution.py
+++ b/solution.py
@@ -71,12 +71,15 @@
     precond_raw = precondition(assembled_load)
     working_raw = operate(precond_raw)
     load_square, cross_first, raw_square = lax.psum(
-        (
-            partial_product(assembled_load, assembled_load),
-            partial_product(working_raw, assembled_load),
-            partial_product(working_raw, working_raw),
+        lax.psum(
+            (
+                partial_product(assembled_load, assembled_load),
+                partial_product(working_raw, assembled_load),
+                partial_product(working_raw, working_raw),
+            ),
+            ("gy", "gz"),
         ),
-        ("gx", "gy", "gz"),
+        "gx",
     )
     initial = jnp.sqrt(load_square + epsilon)
     rescale = 1.0 / initial

time: 335 us -> 316 us (0.943)
  blocking collectives: 86 us -> 67.8 us
    psum x1, blocking collectives: 44 us -> 17 us  [on_device(): lax.psum((partial_product(assembled_load, assembled_load), partial_produc...]
    psum x0 -> x1, blocking collectives: none -> 10.1 us  [on_device(): lax.psum(lax.psum((partial_product(assembled_load, assembled_load), parti...]
where the time goes in v1:
time: 316 us; the launch traced here: 314 us
  local copies, waits for them, and re-layouts  83.5 us (26%)
  starting transfers between devices  78 us (25%)
  blocking collectives  67.8 us (21%)
  other arithmetic  39.6 us (13%)
  matrix products  25.2 us (8%)
  waiting for transfers between devices  18.9 us (6%)
    ppermute x15, starting transfers between devices, extended_2(): before = lax.ppermute(last, axis, up)  58.4 us
    psum x1, blocking collectives, on_device(): lax.psum((partial_product(working, basis_first), partial_product(working,...  40.7 us
    unnamed x50, local copies, waits for them, and re-layouts  22.3 us
    scatter-add x5, other arithmetic, assemble(): extended.at[slot_flat]  21 us
    ppermute x15, starting transfers between devices, extended_2(): after = lax.ppermute(leading, axis, down)  19.6 us
    psum x1, blocking collectives, on_device(): lax.psum((partial_product(assembled_load, assembled_load), partial_produc...  17 us
    concatenate x6, local copies, waits for them, and re-layouts, assemble(): jnp.concatenate([blocks, jnp.zeros((1, block_rows, row_width), jnp.float3...  15.7 us
    dot_general x2, matrix products, operate(): product = jnp.dot(matrix, narrow, preferred_element_type=jnp.float32)  15.7 us
  transfers between devices with their start and end apart: 30, of which 9 were waited for; matrix products, arithmetic and copies ran while one was open for 8% of the time, Pallas kernels for 0%

profile of v1, /device:TPU:0, one launch (start us, length us, event | category | flops | bytes accessed | tf_op | source)
XLA Modules:
  0.0 314.0 jit_solution(14527493924536510107)
XLA Ops:
  7.7 5.6 %collective-permute-start.1 = (f32[1,2,128,256]{3,2,1,0:T(8,128)S(1)}, f32[1,2,128,256]{3,2,1,0:T(8,128)S(1)}, u32[]{:S(2)}, u32[]{:S(2)}) collective-permute-start(f32[1,2,128,256]{3,2,1,0:T(8,128)S(1)} %get-tuple-element.54), channel_id=1, source_target_pairs={{0,8},{8,16},{16,24},{1,9},{9,17},{17,25},{2,10},{10,18},{18,26},{... | collective-permute-start | bytes 786440 | tf_op jit(solution)/shard_map/ppermute | solution.py:16
  17.6 4.4 %collective-permute-start.3 = (f32[1,2,128,256]{3,2,1,0:T(8,128)S(1)}, f32[1,2,128,256]{3,2,1,0:T(8,128)S(1)}, u32[]{:S(2)}, u32[]{:S(2)}) collective-permute-start(f32[1,2,128,256]{3,2,1,0:T(8,128)S(1)} %get-tuple-element.52), channel_id=1, source_target_pairs={{0,2},{2,4},{4,6},{1,3},{3,5},{5,7},{8,10},{10,12},{12,14},{9,11},... | collective-permute-start | bytes 786440 | tf_op jit(solution)/shard_map/ppermute | solution.py:16
  22.1 4.8 %collective-permute-done.2 = f32[1,2,128,256]{3,2,1,0:T(8,128)S(1)} collective-permute-done((f32[1,2,128,256]{3,2,1,0:T(8,128)S(1)}, f32[1,2,128,256]{3,2,1,0:T(8,128)S(1)}, u32[]{:S(2)}, u32[]{:S(2)}) %collective-permute-start.2) | collective-permute-done | bytes 262176 | tf_op jit(solution)/shard_map/ppermute | solution.py:17
  33.0 3.8 %convolution_bitcast_fusion.1 = f32[16,128,256]{1,2,0:T(8,128)S(1)} fusion(f32[17,128,256]{2,1,0:T(8,128)S(1)} %scatter_fusion, f32[1,1,1,16,128,128]{5,4,3,2,1,0:T(8,128)S(1)} %copy-done, f32[16]{0:T(128)S(1)} %convert_element_type.24), kind=kOutput, calls=%fused_computation.32 | convolution fusion | flops 805830656 | bytes 5243392 | tf_op jit(solution)/shard_map/bij,bjr->bir/dot_general | solution.py:57
  38.5 3.4 %gather_fusion.1 = f32[12,128,256]{1,2,0:T(8,128)} fusion(f32[17,128,256]{1,2,0:T(8,128)} %concatenate.19, s32[1024]{0:T(1024)S(1)} %pad_clamp_fusion), kind=kCustom, calls=%fused_computation.1 | custom fusion | bytes 3145776 | tf_op jit(solution)/shard_map/gather | solution.py:27
  45.6 5.3 %collective-permute-start.7 = (f32[1,2,128,256]{2,3,1,0:T(8,128)}, f32[1,2,128,256]{2,3,1,0:T(8,128)}, u32[]{:S(2)}, u32[]{:S(2)}) collective-permute-start(f32[1,2,128,256]{2,3,1,0:T(8,128)} %get-tuple-element.48), channel_id=1, source_target_pairs={{0,8},{8,16},{16,24},{1,9},{9,17},{17,25},{2,10},{10,18},{18,26},{... | collective-permute-start | bytes 786440 | tf_op jit(solution)/shard_map/ppermute | solution.py:16
  57.9 6.6 %collective-permute-start.9 = (f32[1,2,128,256]{2,3,1,0:T(8,128)}, f32[1,2,128,256]{2,3,1,0:T(8,128)S(1)}, u32[]{:S(2)}, u32[]{:S(2)}) collective-permute-start(f32[1,2,128,256]{2,3,1,0:T(8,128)} %get-tuple-element.46), channel_id=1, source_target_pairs={{0,2},{2,4},{4,6},{1,3},{3,5},{5,7},{8,10},{10,12},{12,14},{9,11},... | collective-permute-start | bytes 786440 | tf_op jit(solution)/shard_map/ppermute | solution.py:16
  76.3 4.5 %scatter_fusion.1 = f32[17,128,256]{2,1,0:T(8,128)} fusion(f32[17,128,256]{2,1,0:T(8,128)} %copy.23, s32[12]{0:T(128)S(1)} %fusion.24, f32[12,128,256]{2,1,0:T(8,128)} %copy.24), kind=kCustom, calls=%fused_computation.6 | custom fusion | flops 393216 | bytes 4718640 | tf_op jit(solution)/shard_map/scatter-add | solution.py:34
  80.7 3.6 %fusion.28 = (bf16[16,128,256]{2,1,0:T(8,128)(2,1)}, f32[16,128,256]{2,1,0:T(8,128)}) fusion(f32[16]{0:T(128)S(1)} %convert_element_type.24, f32[17,128,256]{2,1,0:T(8,128)} %scatter_fusion.1), kind=kLoop, calls=%fused_computation.126 | loop fusion | flops 1048576 | bytes 5242944 | tf_op jit(solution)/shard_map/convert_element_type | solution.py:64
  87.3 8.0 %fusion.13 = f32[2048,256]{0,1:T(8,128)} fusion(bf16[2048,256]{1,0:T(8,128)(2,1)} %bitcast.116, bf16[1,1,1,2048,2048]{4,3,2,1,0:T(8,128)(2,1)} %param.5, f32[2048,256]{0,1:T(8,128)} %copy.25, f32[2048]{0:T(1024)S(1)} %bitcast.119), kind=kOutput, calls=%fused_computation.17 | convolution fusion | flops 2148532224 | bytes 13639680 | tf_op jit(solution)/shard_map/dot_general | solution.py:65
  101.4 3.4 %gather_fusion.2 = f32[12,128,256]{2,1,0:T(8,128)} fusion(f32[17,128,256]{2,1,0:T(8,128)} %concatenate.20, s32[1024]{0:T(1024)S(1)} %pad_clamp_fusion), kind=kCustom, calls=%fused_computation.2 | custom fusion | bytes 3145776 | tf_op jit(solution)/shard_map/gather | solution.py:27
  107.6 4.6 %collective-permute-start.13 = (f32[1,2,128,256]{3,2,1,0:T(8,128)S(1)}, f32[1,2,128,256]{3,2,1,0:T(8,128)S(1)}, u32[]{:S(2)}, u32[]{:S(2)}) collective-permute-start(f32[1,2,128,256]{3,2,1,0:T(8,128)S(1)} %get-tuple-element.42), channel_id=1, source_target_pairs={{0,8},{8,16},{16,24},{1,9},{9,17},{17,25},{2,10},{10,18},{18,26},{... | collective-permute-start | bytes 786440 | tf_op jit(solution)/shard_map/ppermute | solution.py:16
  116.8 5.4 %collective-permute-start.15 = (f32[1,2,128,256]{3,2,1,0:T(8,128)S(1)}, f32[1,2,128,256]{3,2,1,0:T(8,128)S(1)}, u32[]{:S(2)}, u32[]{:S(2)}) collective-permute-start(f32[1,2,128,256]{3,2,1,0:T(8,128)S(1)} %get-tuple-element.40), channel_id=1, source_target_pairs={{0,2},{2,4},{4,6},{1,3},{3,5},{5,7},{8,10},{10,12},{12,14},{9,11},... | collective-permute-start | bytes 786440 | tf_op jit(solution)/shard_map/ppermute | solution.py:16
  124.4 4.3 %collective-permute-done.15 = f32[1,2,128,256]{3,2,1,0:T(8,128)S(1)} collective-permute-done((f32[1,2,128,256]{3,2,1,0:T(8,128)S(1)}, f32[1,2,128,256]{3,2,1,0:T(8,128)S(1)}, u32[]{:S(2)}, u32[]{:S(2)}) %collective-permute-start.15) | collective-permute-done | bytes 262176 | tf_op jit(solution)/shard_map/ppermute | solution.py:16
  130.9 4.5 %scatter_fusion.2 = f32[17,128,256]{2,1,0:T(8,128)} fusion(f32[17,128,256]{2,1,0:T(8,128)} %concatenate.20, s32[12]{0:T(128)S(1)} %fusion.24, f32[12,128,256]{2,1,0:T(8,128)} %bitcast.31), kind=kCustom, calls=%fused_computation.7 | custom fusion | flops 393216 | bytes 4718640 | tf_op jit(solution)/shard_map/scatter-add | solution.py:34
  137.7 17.0 %all-reduce.6 = (f32[256]{0:T(256)S(1)}, f32[256]{0:T(256)S(1)}, f32[256]{0:T(256)S(1)}) all-reduce(f32[256]{0:T(256)S(1)} %broadcast_multiply_fusion.5, f32[256]{0:T(256)S(1)} %get-tuple-element.57, f32[256]{0:T(256)S(1)} %get-tuple-element.58), channel_id=1, replica_groups=mesh['gx'=4,'gy'=4,'gz'=2] {'gy','gz'}, use_global_device_ids=true, to_apply=%region_3.0 | all-reduce | flops 768 | bytes 6144 | tf_op jit(solution)/shard_map/psum | solution.py:74
  154.6 10.1 %all-reduce.7 = (f32[256]{0:T(256)S(1)}, f32[256]{0:T(256)S(1)}, f32[256]{0:T(256)S(1)}) all-reduce(f32[256]{0:T(256)S(1)} %get-tuple-element.11, f32[256]{0:T(256)S(1)} %get-tuple-element.12, f32[256]{0:T(256)S(1)} %get-tuple-element.13), channel_id=1, replica_groups=mesh['gx'=4,'gy'=4,'gz'=2] {'gx'}, use_global_device_ids=true, to_apply=%region_4.0 | all-reduce | flops 768 | bytes 6144 | tf_op jit(solution)/shard_map/psum | solution.py:73
  164.8 5.7 %convolution_bitcast_fusion = f32[16,128,256]{1,2,0:T(8,128)S(1)} fusion(f32[1,1,1,16,128,128]{5,4,3,2,1,0:T(8,128)S(1)} %copy-done, f32[17,128,256]{2,1,0:T(8,128)} %scatter_fusion.2, f32[17,128,256]{2,1,0:T(8,128)S(1)} %scatter_fusion, f32[256]{0:T(256)S(1)} %get-tuple-element.21, f32[256]{0:T(256)S(1)} %get-tuple-element.22, ...), kind=kOutput, calls=%fused_computation.31 | convolution fusion | flops 808976384 | bytes 7343616 | tf_op jit(solution)/shard_map/bij,bjr->bir/dot_general | solution.py:57
  172.1 3.4 %gather_fusion.3 = f32[12,128,256]{1,2,0:T(8,128)} fusion(f32[17,128,256]{1,2,0:T(8,128)} %concatenate.21, s32[1024]{0:T(1024)S(1)} %pad_clamp_fusion), kind=kCustom, calls=%fused_computation.3 | custom fusion | bytes 3145776 | tf_op jit(solution)/shard_map/gather | solution.py:27
  179.2 5.3 %collective-permute-start.19 = (f32[1,2,128,256]{2,3,1,0:T(8,128)S(1)}, f32[1,2,128,256]{2,3,1,0:T(8,128)}, u32[]{:S(2)}, u32[]{:S(2)}) collective-permute-start(f32[1,2,128,256]{2,3,1,0:T(8,128)S(1)} %get-tuple-element.36), channel_id=1, source_target_pairs={{0,8},{8,16},{16,24},{1,9},{9,17},{17,25},{2,10},{10,18},{18,26},{... | collective-permute-start | bytes 786440 | tf_op jit(solution)/shard_map/ppermute | solution.py:16
  191.4 4.6 %collective-permute-start.21 = (f32[1,2,128,256]{2,3,1,0:T(8,128)S(1)}, f32[1,2,128,256]{2,3,1,0:T(8,128)S(1)}, u32[]{:S(2)}, u32[]{:S(2)}) collective-permute-start(f32[1,2,128,256]{2,3,1,0:T(8,128)S(1)} %get-tuple-element.34), channel_id=1, source_target_pairs={{0,2},{2,4},{4,6},{1,3},{3,5},{5,7},{8,10},{10,12},{12,14},{9,11},... | collective-permute-start | bytes 786440 | tf_op jit(solution)/shard_map/ppermute | solution.py:16
  207.7 4.5 %scatter_fusion.3 = f32[17,128,256]{2,1,0:T(8,128)} fusion(f32[17,128,256]{2,1,0:T(8,128)} %copy.28, s32[12]{0:T(128)S(1)} %fusion.24, f32[12,128,256]{2,1,0:T(8,128)} %copy.29), kind=kCustom, calls=%fused_computation.8 | custom fusion | flops 393216 | bytes 4718640 | tf_op jit(solution)/shard_map/scatter-add | solution.py:34
  212.2 3.3 %fusion.27 = (bf16[16,128,256]{2,1,0:T(8,128)(2,1)S(1)}, f32[16,128,256]{2,1,0:T(8,128)}) fusion(f32[16]{0:T(128)S(1)} %convert_element_type.24, f32[17,128,256]{2,1,0:T(8,128)} %scatter_fusion.3), kind=kLoop, calls=%fused_computation.125 | loop fusion | flops 1048576 | bytes 5242944 | tf_op jit(solution)/shard_map/convert_element_type | solution.py:64
  218.4 7.7 %fusion.10 = f32[2048,256]{0,1:T(8,128)} fusion(bf16[2048,256]{1,0:T(8,128)(2,1)S(1)} %bitcast.117, bf16[1,1,1,2048,2048]{4,3,2,1,0:T(8,128)(2,1)} %param.5, f32[2048,256]{0,1:T(8,128)} %copy.30, f32[2048]{0:T(1024)S(1)} %bitcast.120), kind=kOutput, calls=%fused_computation.16 | convolution fusion | flops 2148532224 | bytes 13639680 | tf_op jit(solution)/shard_map/dot_general | solution.py:65
  232.4 3.4 %gather_fusion.4 = f32[12,128,256]{2,1,0:T(8,128)} fusion(f32[17,128,256]{2,1,0:T(8,128)} %concatenate.22, s32[1024]{0:T(1024)S(1)} %pad_clamp_fusion), kind=kCustom, calls=%fused_computation.4 | custom fusion | bytes 3145776 | tf_op jit(solution)/shard_map/gather | solution.py:27
  238.6 4.6 %collective-permute-start.25 = (f32[1,2,128,256]{3,2,1,0:T(8,128)S(1)}, f32[1,2,128,256]{3,2,1,0:T(8,128)S(1)}, u32[]{:S(2)}, u32[]{:S(2)}) collective-permute-start(f32[1,2,128,256]{3,2,1,0:T(8,128)S(1)} %get-tuple-element.30), channel_id=1, source_target_pairs={{0,8},{8,16},{16,24},{1,9},{9,17},{17,25},{2,10},{10,18},{18,26},{... | collective-permute-start | bytes 786440 | tf_op jit(solution)/shard_map/ppermute | solution.py:16
  247.7 4.5 %collective-permute-start.27 = (f32[1,2,128,256]{3,2,1,0:T(8,128)S(1)}, f32[1,2,128,256]{3,2,1,0:T(8,128)S(1)}, u32[]{:S(2)}, u32[]{:S(2)}) collective-permute-start(f32[1,2,128,256]{3,2,1,0:T(8,128)S(1)} %get-tuple-element.28), channel_id=1, source_target_pairs={{0,2},{2,4},{4,6},{1,3},{3,5},{5,7},{8,10},{10,12},{12,14},{9,11},... | collective-permute-start | bytes 786440 | tf_op jit(solution)/shard_map/ppermute | solution.py:16
  254.5 4.3 %collective-permute-done.27 = f32[1,2,128,256]{3,2,1,0:T(8,128)S(1)} collective-permute-done((f32[1,2,128,256]{3,2,1,0:T(8,128)S(1)}, f32[1,2,128,256]{3,2,1,0:T(8,128)S(1)}, u32[]{:S(2)}, u32[]{:S(2)}) %collective-permute-start.27) | collective-permute-done | bytes 262176 | tf_op jit(solution)/shard_map/ppermute | solution.py:16
  261.0 4.5 %scatter_fusion.4 = f32[17,128,256]{2,1,0:T(8,128)} fusion(f32[17,128,256]{2,1,0:T(8,128)} %concatenate.22, s32[12]{0:T(128)S(1)} %fusion.24, f32[12,128,256]{2,1,0:T(8,128)} %bitcast.50), kind=kCustom, calls=%fused_computation.9 | custom fusion | flops 393216 | bytes 4718640 | tf_op jit(solution)/shard_map/scatter-add | solution.py:34
  265.4 3.2 %multiply_reduce_fusion.2 = (f32[256]{0:T(256)S(1)}, f32[256]{0:T(256)S(1)}, f32[256]{0:T(256)S(1)}) fusion(f32[17,128,256]{2,1,0:T(8,128)} %scatter_fusion.4, f32[17,128,256]{2,1,0:T(8,128)S(1)} %scatter_fusion, f32[256]{0:T(256)S(1)} %get-tuple-element.23, f32[16]{0:T(128)S(1)} %convert_element_type.24, f32[256]{0:T(256)S(1)} %copy-done.4, ...), kind=kLoop, calls=%fused_computation.26 | loop fusion | flops 7339264 | bytes 6297664 | tf_op jit(solution)/shard_map/reduce_sum | solution.py:39
  268.7 40.7 %all-reduce.5 = (f32[256]{0:T(256)S(1)}, f32[256]{0:T(256)S(1)}, f32[256]{0:T(256)S(1)}) all-reduce(f32[256]{0:T(256)S(1)} %broadcast_multiply_fusion.1, f32[256]{0:T(256)S(1)} %broadcast_multiply_fusion, f32[256]{0:T(256)S(1)} %broadcast_multiply_fusion.2), channel_id=1, replica_groups=mesh['gx'=4,'gy'=4,'gz'=2] {'gx','gy','gz'}, use_global_device_ids=true, to_apply=%region_18.0 | all-reduce | flops 768 | bytes 6144 | tf_op jit(solution)/shard_map/psum | solution.py:96
  310.0 4.0 %multiply_add_fusion = f32[16,128,256]{2,1,0:T(8,128)} fusion(f32[16,128,256]{2,1,0:T(8,128)} %get-tuple-element.20, f32[16,128,256]{2,1,0:T(8,128)} %get-tuple-element.25, f32[256]{0:T(256)S(1)} %get-tuple-element.18, f32[256]{0:T(256)S(1)} %get-tuple-element.17, f32[256]{0:T(256)S(1)} %get-tuple-element.23), kind=kLoop, calls=%fused_computation.23 | loop fusion | flops 2097152 | bytes 6294528 | tf_op jit(solution)/shard_map/add | solution.py:118
  (135 shorter events, 110.0 us)
Async XLA Ops:
  0.6 32.4 %copy-start = (f32[1,1,1,16,128,128]{5,4,3,2,1,0:T(8,128)S(1)}, f32[1,1,1,16,128,128]{5,4,3,2,1,0:T(8,128)}, u32[]{:S(2)}) copy-start(f32[1,1,1,16,128,128]{5,4,3,2,1,0:T(8,128)} %param.7) | copy-start | bytes 3145732
  6.4 11.3 %collective-permute-start = (f32[1,2,128,256]{3,2,1,0:T(8,128)S(1)}, f32[1,2,128,256]{3,2,1,0:T(8,128)S(1)}, u32[]{:S(2)}, u32[]{:S(2)}) collective-permute-start(f32[1,2,128,256]{3,2,1,0:T(8,128)S(1)} %get-tuple-element.55), channel_id=1, source_target_pairs={{8,0},{16,8},{24,16},{9,1},{17,9},{25,17},{10,2},{18,10},{26,18},{... | collective-permute-start | bytes 786440 | tf_op jit(solution)/shard_map/ppermute | solution.py:17
  7.7 14.4 %collective-permute-start.1 = (f32[1,2,128,256]{3,2,1,0:T(8,128)S(1)}, f32[1,2,128,256]{3,2,1,0:T(8,128)S(1)}, u32[]{:S(2)}, u32[]{:S(2)}) collective-permute-start(f32[1,2,128,256]{3,2,1,0:T(8,128)S(1)} %get-tuple-element.54), channel_id=1, source_target_pairs={{0,8},{8,16},{16,24},{1,9},{9,17},{17,25},{2,10},{10,18},{18,26},{... | collective-permute-start | bytes 786440 | tf_op jit(solution)/shard_map/ppermute | solution.py:16
  13.3 15.4 %collective-permute-start.5 = (f32[1,2,128,256]{3,2,1,0:T(8,128)S(1)}, f32[1,2,128,256]{3,2,1,0:T(8,128)S(1)}, u32[]{:S(2)}, u32[]{:S(2)}) collective-permute-start(f32[1,2,128,256]{3,2,1,0:T(8,128)S(1)} %get-tuple-element.50), channel_id=1, source_target_pairs={{0,1},{2,3},{4,5},{6,7},{8,9},{10,11},{12,13},{14,15},{16,17},{18,... | collective-permute-start | bytes 786440 | tf_op jit(solution)/shard_map/ppermute | solution.py:16
  14.8 13.9 %collective-permute-start.4 = (f32[1,2,128,256]{3,2,1,0:T(8,128)S(1)}, f32[1,2,128,256]{3,2,1,0:T(8,128)S(1)}, u32[]{:S(2)}, u32[]{:S(2)}) collective-permute-start(f32[1,2,128,256]{3,2,1,0:T(8,128)S(1)} %get-tuple-element.51), channel_id=1, source_target_pairs={{1,0},{3,2},{5,4},{7,6},{9,8},{11,10},{13,12},{15,14},{17,16},{19,... | collective-permute-start | bytes 786440 | tf_op jit(solution)/shard_map/ppermute | solution.py:17
  16.1 10.9 %collective-permute-start.2 = (f32[1,2,128,256]{3,2,1,0:T(8,128)S(1)}, f32[1,2,128,256]{3,2,1,0:T(8,128)S(1)}, u32[]{:S(2)}, u32[]{:S(2)}) collective-permute-start(f32[1,2,128,256]{3,2,1,0:T(8,128)S(1)} %get-tuple-element.53), channel_id=1, source_target_pairs={{2,0},{4,2},{6,4},{3,1},{5,3},{7,5},{10,8},{12,10},{14,12},{11,9},... | collective-permute-start | bytes 786440 | tf_op jit(solution)/shard_map/ppermute | solution.py:17
  17.6 11.0 %collective-permute-start.3 = (f32[1,2,128,256]{3,2,1,0:T(8,128)S(1)}, f32[1,2,128,256]{3,2,1,0:T(8,128)S(1)}, u32[]{:S(2)}, u32[]{:S(2)}) collective-permute-start(f32[1,2,128,256]{3,2,1,0:T(8,128)S(1)} %get-tuple-element.52), channel_id=1, source_target_pairs={{0,2},{2,4},{4,6},{1,3},{3,5},{5,7},{8,10},{10,12},{12,14},{9,11},... | collective-permute-start | bytes 786440 | tf_op jit(solution)/shard_map/ppermute | solution.py:16
  44.3 13.6 %collective-permute-start.6 = (f32[1,2,128,256]{2,3,1,0:T(8,128)}, f32[1,2,128,256]{2,3,1,0:T(8,128)}, u32[]{:S(2)}, u32[]{:S(2)}) collective-permute-start(f32[1,2,128,256]{2,3,1,0:T(8,128)} %get-tuple-element.49), channel_id=1, source_target_pairs={{8,0},{16,8},{24,16},{9,1},{17,9},{25,17},{10,2},{18,10},{26,18},{... | collective-permute-start | bytes 786440 | tf_op jit(solution)/shard_map/ppermute | solution.py:17
  45.6 20.5 %collective-permute-start.7 = (f32[1,2,128,256]{2,3,1,0:T(8,128)}, f32[1,2,128,256]{2,3,1,0:T(8,128)}, u32[]{:S(2)}, u32[]{:S(2)}) collective-permute-start(f32[1,2,128,256]{2,3,1,0:T(8,128)} %get-tuple-element.48), channel_id=1, source_target_pairs={{0,8},{8,16},{16,24},{1,9},{9,17},{17,25},{2,10},{10,18},{18,26},{... | collective-permute-start | bytes 786440 | tf_op jit(solution)/shard_map/ppermute | solution.py:16
  50.9 17.0 %collective-permute-start.8 = (f32[1,2,128,256]{2,3,1,0:T(8,128)}, f32[1,2,128,256]{2,3,1,0:T(8,128)}, u32[]{:S(2)}, u32[]{:S(2)}) collective-permute-start(f32[1,2,128,256]{2,3,1,0:T(8,128)} %get-tuple-element.47), channel_id=1, source_target_pairs={{2,0},{4,2},{6,4},{3,1},{5,3},{7,5},{10,8},{12,10},{14,12},{11,9},... | collective-permute-start | bytes 786440 | tf_op jit(solution)/shard_map/ppermute | solution.py:17
  55.2 17.4 %collective-permute-start.11 = (f32[1,2,128,256]{2,3,1,0:T(8,128)S(1)}, f32[1,2,128,256]{2,3,1,0:T(8,128)S(1)}, u32[]{:S(2)}, u32[]{:S(2)}) collective-permute-start(f32[1,2,128,256]{2,3,1,0:T(8,128)S(1)} %get-tuple-element.44), channel_id=1, source_target_pairs={{0,1},{2,3},{4,5},{6,7},{8,9},{10,11},{12,13},{14,15},{16,17},{18,... | collective-permute-start | bytes 786440 | tf_op jit(solution)/shard_map/ppermute | solution.py:16
  56.6 15.2 %collective-permute-start.10 = (f32[1,2,128,256]{2,3,1,0:T(8,128)}, f32[1,2,128,256]{2,3,1,0:T(8,128)S(1)}, u32[]{:S(2)}, u32[]{:S(2)}) collective-permute-start(f32[1,2,128,256]{2,3,1,0:T(8,128)} %get-tuple-element.45), channel_id=1, source_target_pairs={{1,0},{3,2},{5,4},{7,6},{9,8},{11,10},{13,12},{15,14},{17,16},{19,... | collective-permute-start | bytes 786440 | tf_op jit(solution)/shard_map/ppermute | solution.py:17
  57.9 13.2 %collective-permute-start.9 = (f32[1,2,128,256]{2,3,1,0:T(8,128)}, f32[1,2,128,256]{2,3,1,0:T(8,128)S(1)}, u32[]{:S(2)}, u32[]{:S(2)}) collective-permute-start(f32[1,2,128,256]{2,3,1,0:T(8,128)} %get-tuple-element.46), channel_id=1, source_target_pairs={{0,2},{2,4},{4,6},{1,3},{3,5},{5,7},{8,10},{10,12},{12,14},{9,11},... | collective-permute-start | bytes 786440 | tf_op jit(solution)/shard_map/ppermute | solution.py:16
  106.3 10.5 %collective-permute-start.12 = (f32[1,2,128,256]{3,2,1,0:T(8,128)S(1)}, f32[1,2,128,256]{3,2,1,0:T(8,128)S(1)}, u32[]{:S(2)}, u32[]{:S(2)}) collective-permute-start(f32[1,2,128,256]{3,2,1,0:T(8,128)S(1)} %get-tuple-element.43), channel_id=1, source_target_pairs={{8,0},{16,8},{24,16},{9,1},{17,9},{25,17},{10,2},{18,10},{26,18},{... | collective-permute-start | bytes 786440 | tf_op jit(solution)/shard_map/ppermute | solution.py:17
  107.6 15.4 %collective-permute-start.13 = (f32[1,2,128,256]{3,2,1,0:T(8,128)S(1)}, f32[1,2,128,256]{3,2,1,0:T(8,128)S(1)}, u32[]{:S(2)}, u32[]{:S(2)}) collective-permute-start(f32[1,2,128,256]{3,2,1,0:T(8,128)S(1)} %get-tuple-element.42), channel_id=1, source_target_pairs={{0,8},{8,16},{16,24},{1,9},{9,17},{17,25},{2,10},{10,18},{18,26},{... | collective-permute-start | bytes 786440 | tf_op jit(solution)/shard_map/ppermute | solution.py:16
  112.2 11.5 %collective-permute-start.14 = (f32[1,2,128,256]{3,2,1,0:T(8,128)S(1)}, f32[1,2,128,256]{3,2,1,0:T(8,128)S(1)}, u32[]{:S(2)}, u32[]{:S(2)}) collective-permute-start(f32[1,2,128,256]{3,2,1,0:T(8,128)S(1)} %get-tuple-element.41), channel_id=1, source_target_pairs={{2,0},{4,2},{6,4},{3,1},{5,3},{7,5},{10,8},{12,10},{14,12},{11,9},... | collective-permute-start | bytes 786440 | tf_op jit(solution)/shard_map/ppermute | solution.py:17
  113.5 16.7 %collective-permute-start.17 = (f32[1,2,128,256]{3,2,1,0:T(8,128)S(1)}, f32[1,2,128,256]{3,2,1,0:T(8,128)S(1)}, u32[]{:S(2)}, u32[]{:S(2)}) collective-permute-start(f32[1,2,128,256]{3,2,1,0:T(8,128)S(1)} %get-tuple-element.38), channel_id=1, source_target_pairs={{0,1},{2,3},{4,5},{6,7},{8,9},{10,11},{12,13},{14,15},{16,17},{18,... | collective-permute-start | bytes 786440 | tf_op jit(solution)/shard_map/ppermute | solution.py:16
  115.2 14.2 %collective-permute-start.16 = (f32[1,2,128,256]{3,2,1,0:T(8,128)S(1)}, f32[1,2,128,256]{3,2,1,0:T(8,128)S(1)}, u32[]{:S(2)}, u32[]{:S(2)}) collective-permute-start(f32[1,2,128,256]{3,2,1,0:T(8,128)S(1)} %get-tuple-element.39), channel_id=1, source_target_pairs={{1,0},{3,2},{5,4},{7,6},{9,8},{11,10},{13,12},{15,14},{17,16},{19,... | collective-permute-start | bytes 786440 | tf_op jit(solution)/shard_map/ppermute | solution.py:17
  116.8 11.9 %collective-permute-start.15 = (f32[1,2,128,256]{3,2,1,0:T(8,128)S(1)}, f32[1,2,128,256]{3,2,1,0:T(8,128)S(1)}, u32[]{:S(2)}, u32[]{:S(2)}) collective-permute-start(f32[1,2,128,256]{3,2,1,0:T(8,128)S(1)} %get-tuple-element.40), channel_id=1, source_target_pairs={{0,2},{2,4},{4,6},{1,3},{3,5},{5,7},{8,10},{10,12},{12,14},{9,11},... | collective-permute-start | bytes 786440 | tf_op jit(solution)/shard_map/ppermute | solution.py:16
  177.7 13.7 %collective-permute-start.18 = (f32[1,2,128,256]{2,3,1,0:T(8,128)}, f32[1,2,128,256]{2,3,1,0:T(8,128)}, u32[]{:S(2)}, u32[]{:S(2)}) collective-permute-start(f32[1,2,128,256]{2,3,1,0:T(8,128)} %get-tuple-element.37), channel_id=1, source_target_pairs={{8,0},{16,8},{24,16},{9,1},{17,9},{25,17},{10,2},{18,10},{26,18},{... | collective-permute-start | bytes 786440 | tf_op jit(solution)/shard_map/ppermute | solution.py:17
  179.2 18.4 %collective-permute-start.19 = (f32[1,2,128,256]{2,3,1,0:T(8,128)S(1)}, f32[1,2,128,256]{2,3,1,0:T(8,128)}, u32[]{:S(2)}, u32[]{:S(2)}) collective-permute-start(f32[1,2,128,256]{2,3,1,0:T(8,128)S(1)} %get-tuple-element.36), channel_id=1, source_target_pairs={{0,8},{8,16},{16,24},{1,9},{9,17},{17,25},{2,10},{10,18},{18,26},{... | collective-permute-start | bytes 786440 | tf_op jit(solution)/shard_map/ppermute | solution.py:16
  184.5 14.9 %collective-permute-start.20 = (f32[1,2,128,256]{2,3,1,0:T(8,128)S(1)}, f32[1,2,128,256]{2,3,1,0:T(8,128)}, u32[]{:S(2)}, u32[]{:S(2)}) collective-permute-start(f32[1,2,128,256]{2,3,1,0:T(8,128)S(1)} %get-tuple-element.35), channel_id=1, source_target_pairs={{2,0},{4,2},{6,4},{3,1},{5,3},{7,5},{10,8},{12,10},{14,12},{11,9},... | collective-permute-start | bytes 786440 | tf_op jit(solution)/shard_map/ppermute | solution.py:17
  188.8 15.2 %collective-permute-start.23 = (f32[1,2,128,256]{2,3,1,0:T(8,128)S(1)}, f32[1,2,128,256]{2,3,1,0:T(8,128)S(1)}, u32[]{:S(2)}, u32[]{:S(2)}) collective-permute-start(f32[1,2,128,256]{2,3,1,0:T(8,128)S(1)} %get-tuple-element.32), channel_id=1, source_target_pairs={{0,1},{2,3},{4,5},{6,7},{8,9},{10,11},{12,13},{14,15},{16,17},{18,... | collective-permute-start | bytes 786440 | tf_op jit(solution)/shard_map/ppermute | solution.py:16
  190.1 13.1 %collective-permute-start.22 = (f32[1,2,128,256]{2,3,1,0:T(8,128)S(1)}, f32[1,2,128,256]{2,3,1,0:T(8,128)S(1)}, u32[]{:S(2)}, u32[]{:S(2)}) collective-permute-start(f32[1,2,128,256]{2,3,1,0:T(8,128)S(1)} %get-tuple-element.33), channel_id=1, source_target_pairs={{1,0},{3,2},{5,4},{7,6},{9,8},{11,10},{13,12},{15,14},{17,16},{19,... | collective-permute-start | bytes 786440 | tf_op jit(solution)/shard_map/ppermute | solution.py:17
  191.4 11.1 %collective-permute-start.21 = (f32[1,2,128,256]{2,3,1,0:T(8,128)S(1)}, f32[1,2,128,256]{2,3,1,0:T(8,128)S(1)}, u32[]{:S(2)}, u32[]{:S(2)}) collective-permute-start(f32[1,2,128,256]{2,3,1,0:T(8,128)S(1)} %get-tuple-element.34), channel_id=1, source_target_pairs={{0,2},{2,4},{4,6},{1,3},{3,5},{5,7},{8,10},{10,12},{12,14},{9,11},... | collective-permute-start | bytes 786440 | tf_op jit(solution)/shard_map/ppermute | solution.py:16
  237.3 10.5 %collective-permute-start.24 = (f32[1,2,128,256]{3,2,1,0:T(8,128)S(1)}, f32[1,2,128,256]{3,2,1,0:T(8,128)S(1)}, u32[]{:S(2)}, u32[]{:S(2)}) collective-permute-start(f32[1,2,128,256]{3,2,1,0:T(8,128)S(1)} %get-tuple-element.31), channel_id=1, source_target_pairs={{8,0},{16,8},{24,16},{9,1},{17,9},{25,17},{10,2},{18,10},{26,18},{... | collective-permute-start | bytes 786440 | tf_op jit(solution)/shard_map/ppermute | solution.py:17
  238.6 14.5 %collective-permute-start.25 = (f32[1,2,128,256]{3,2,1,0:T(8,128)S(1)}, f32[1,2,128,256]{3,2,1,0:T(8,128)S(1)}, u32[]{:S(2)}, u32[]{:S(2)}) collective-permute-start(f32[1,2,128,256]{3,2,1,0:T(8,128)S(1)} %get-tuple-element.30), channel_id=1, source_target_pairs={{0,8},{8,16},{16,24},{1,9},{9,17},{17,25},{2,10},{10,18},{18,26},{... | collective-permute-start | bytes 786440 | tf_op jit(solution)/shard_map/ppermute | solution.py:16
  243.1 10.6 %collective-permute-start.26 = (f32[1,2,128,256]{3,2,1,0:T(8,128)S(1)}, f32[1,2,128,256]{3,2,1,0:T(8,128)S(1)}, u32[]{:S(2)}, u32[]{:S(2)}) collective-permute-start(f32[1,2,128,256]{3,2,1,0:T(8,128)S(1)} %get-tuple-element.29), channel_id=1, source_target_pairs={{2,0},{4,2},{6,4},{3,1},{5,3},{7,5},{10,8},{12,10},{14,12},{11,9},... | collective-permute-start | bytes 786440 | tf_op jit(solution)/shard_map/ppermute | solution.py:17
  244.4 15.8 %collective-permute-start.29 = (f32[1,2,128,256]{3,2,1,0:T(8,128)S(1)}, f32[1,2,128,256]{3,2,1,0:T(8,128)S(1)}, u32[]{:S(2)}, u32[]{:S(2)}) collective-permute-start(f32[1,2,128,256]{3,2,1,0:T(8,128)S(1)} %get-tuple-element.26), channel_id=1, source_target_pairs={{0,1},{2,3},{4,5},{6,7},{8,9},{10,11},{12,13},{14,15},{16,17},{18,... | collective-permute-start | bytes 786440 | tf_op jit(solution)/shard_map/ppermute | solution.py:16
  246.2 13.3 %collective-permute-start.28 = (f32[1,2,128,256]{3,2,1,0:T(8,128)S(1)}, f32[1,2,128,256]{3,2,1,0:T(8,128)S(1)}, u32[]{:S(2)}, u32[]{:S(2)}) collective-permute-start(f32[1,2,128,256]{3,2,1,0:T(8,128)S(1)} %get-tuple-element.27), channel_id=1, source_target_pairs={{1,0},{3,2},{5,4},{7,6},{9,8},{11,10},{13,12},{15,14},{17,16},{19,... | collective-permute-start | bytes 786440 | tf_op jit(solution)/shard_map/ppermute | solution.py:17
  247.7 11.0 %collective-permute-start.27 = (f32[1,2,128,256]{3,2,1,0:T(8,128)S(1)}, f32[1,2,128,256]{3,2,1,0:T(8,128)S(1)}, u32[]{:S(2)}, u32[]{:S(2)}) collective-permute-start(f32[1,2,128,256]{3,2,1,0:T(8,128)S(1)} %get-tuple-element.28), channel_id=1, source_target_pairs={{0,2},{2,4},{4,6},{1,3},{3,5},{5,7},{8,10},{10,12},{12,14},{9,11},... | collective-permute-start | bytes 786440 | tf_op jit(solution)/shard_map/ppermute | solution.py:16
  265.4 44.0 %copy-start.8 = (f32[256]{0:T(256)S(1)}, f32[256]{0:T(256)}, u32[]{:S(2)}) copy-start(f32[256]{0:T(256)} %copy-done.7) | copy-start | bytes 3076
  (10 other events, 49.6 us)
